TPU v7x, 32 devices: a 4x2x2 block of a 4x4x8 slice. The times are simulated.
32 devices in a mesh: dp: 4 (over y, z), sp: 8 (over x, core).
Axes of the slice: x: 4, y: 2, z: 2, core: 2. Of those that a mesh axis runs over, the one named last changes fastest.
The devices are a block of a 4x4x8 slice.
Arguments:
- image_tokens: bfloat16 [64, 1024, 1152], P('dp', 'sp'), parts along dimension 0
- ln1_gain: float32 [2, 1152], replicated
- ln1_shift: float32 [2, 1152], replicated
- w_qkv: bfloat16 [2, 1152, 3, 16, 72], replicated
- b_qkv: float32 [2, 3, 16, 72], replicated
- w_out: bfloat16 [2, 16, 72, 1152], replicated
- b_out: float32 [2, 1152], replicated
- ln2_gain: float32 [2, 1152], replicated
- ln2_shift: float32 [2, 1152], replicated
- w_up: bfloat16 [2, 1152, 4304], replicated
- b_up: float32 [2, 4304], replicated
- w_down: bfloat16 [2, 4304, 1152], replicated
- b_down: float32 [2, 1152], replicated
Outputs:
- output: bfloat16 [64, 1024, 1152], P('dp', 'sp'), parts along dimension 0
There are 4 independent parts. A program takes and returns all parts, laid end to end along the dimension named above; an argument that names none is the same for every part.
All inputs are finite; a program needn't handle non-finite values.
Results may differ from a plain program's by a relative error of at most 0.0143792.
Values are sent between devices in bfloat16 or wider.
A program may use at most 768 MiB of HBM per device.

v0:
```python
import jax
import jax.numpy as jnp
from jax import lax
from jax.sharding import PartitionSpec as P

LN_EPS = 1e-6


def layer_norm(tokens, ln_gain, ln_shift):
    values = tokens.astype(jnp.float32)
    mean_val = jnp.mean(values, axis=-1, keepdims=True)
    centred = values - mean_val
    var_val = jnp.mean(centred * centred, axis=-1, keepdims=True)
    return (centred * lax.rsqrt(var_val + LN_EPS) * ln_gain + ln_shift).astype(jnp.bfloat16)


def attend(q_part, k_part, v_part):
    score_scale = q_part.shape[-1] ** -0.5
    scores = jnp.einsum('bqhe,bkhe->bhqk', q_part, k_part, preferred_element_type=jnp.float32) * score_scale
    row_peak = jnp.max(scores, axis=-1, keepdims=True)
    prob_vals = jnp.exp(scores - row_peak)
    row_total = jnp.sum(prob_vals, axis=-1, keepdims=True)
    mixed_vals = jnp.einsum('bhqk,bkhe->bhqe', prob_vals.astype(jnp.bfloat16), v_part, preferred_element_type=jnp.float32)
    return (mixed_vals / row_total).astype(jnp.bfloat16)


def mlp_block(mid_state, ln2_gain, ln2_shift, w_up, b_up, w_down, b_down):
    normed = layer_norm(mid_state, ln2_gain, ln2_shift)
    up_proj = jnp.einsum('bsd,df->bsf', normed, w_up, preferred_element_type=jnp.float32) + b_up
    active = jax.nn.gelu(up_proj, approximate=True).astype(jnp.bfloat16)
    down_proj = jnp.einsum('bsf,fd->bsd', active, w_down, preferred_element_type=jnp.float32) + b_down
    return (mid_state.astype(jnp.float32) + down_proj).astype(jnp.bfloat16)


def solution(mesh):
    token_spec = P('dp', 'sp', None)

    def device_step(image_tokens, ln1_gain, ln1_shift, w_qkv, b_qkv, w_out, b_out, ln2_gain, ln2_shift, w_up, b_up, w_down, b_down):
        hidden = image_tokens
        for layer_idx in range(w_qkv.shape[0]):
            normed = layer_norm(hidden, ln1_gain[layer_idx], ln1_shift[layer_idx])
            qkv_local = (jnp.einsum('bsd,dthe->bsthe', normed, w_qkv[layer_idx], preferred_element_type=jnp.float32) + b_qkv[layer_idx]).astype(jnp.bfloat16)
            qkv_heads = lax.all_to_all(qkv_local, 'sp', 3, 1, tiled=True)
            attn_heads = attend(qkv_heads[:, :, 0], qkv_heads[:, :, 1], qkv_heads[:, :, 2])
            attn_tokens = lax.all_to_all(attn_heads, 'sp', 2, 1, tiled=True)
            attn_proj = jnp.einsum('bhse,hed->bsd', attn_tokens, w_out[layer_idx], preferred_element_type=jnp.float32) + b_out[layer_idx]
            mid_state = (hidden.astype(jnp.float32) + attn_proj).astype(jnp.bfloat16)
            hidden = mlp_block(mid_state, ln2_gain[layer_idx], ln2_shift[layer_idx], w_up[layer_idx], b_up[layer_idx], w_down[layer_idx], b_down[layer_idx])
        return hidden

    return jax.shard_map(device_step, mesh=mesh, in_specs=(token_spec,) + (P(),) * 12, out_specs=token_spec, check_vma=False)
```

profile of v0, /device:TPU:81, one launch (start us, length us, event | category | flops | bytes accessed | tf_op | source)
XLA Modules:
  0.0 1165.8 jit_solution(12318563027837752532)
XLA Ops:
  0.0 3.2 convert_reduce_fusion.3
  3.2 3.7 fusion.58
  8.2 25.0 %add_convert_fusion.1 = bf16[16,128,3,16,72]{1,4,3,2,0:T(8,128)(2,1)} fusion(f32[3,16,72]{2,1,0:T(8,128)S(1)} %get-tuple-element.20, bf16[2,1152,3,16,72]{1,4,3,2,0:T(8,128)(2,1)} %param.16, bf16[16,128,1152]{2,1,0:T(8,128)(2,1)S(1)} %copy-done, f32[1152]{0:T(1024)S(1)} %get-tuple-element.18, f32[1152]{0:T(1024)S(1)} %get-tuple-element.31, ...), kind=kOutput, calls=%fused_computation.29 | convolution fusion | flops 16335765504 | bytes 26876416 | tf_op jit(solution)/shard_map/bsd,dthe->bsthe/dot_general | solution.py:42
  33.2 6.7 copy.20
  39.9 161.6 %all_to_all.72 = bf16[16,128,3,16,72]{1,4,2,0,3:T(8,128)(2,1)S(1)} all-to-all(bf16[16,128,3,16,72]{1,4,2,0,3:T(8,128)(2,1)S(1)} %copy.20), channel_id=1, replica_groups=mesh['dp'=4,'sp'=8] {'sp'}, dimensions={3} | all-to-all | bytes 28311552 | tf_op jit(solution)/shard_map/all_to_all | solution.py:43
  201.5 10.7 copy.39
  212.2 21.6 %all_to_all.55 = bf16[16,1024,3,2,72]{1,4,3,0,2:T(8,128)(2,1)} reshape(bf16[16,8,128,3,2,72]{2,1,5,4,0,3:T(8,128)(2,1)} %bitcast.127) | data formatting | bytes 28311552 | tf_op jit(solution)/shard_map/all_to_all | solution.py:43
  233.8 47.3 %multiply_reduce_fusion.1 = (f32[16,2,1024]{2,1,0:T(2,128)S(1)}, f32[16,2,1024,1024]{2,3,1,0:T(8,128)}) fusion(bf16[16,1024,3,2,72]{1,4,3,0,2:T(8,128)(2,1)} %all_to_all.55), kind=kOutput, calls=%fused_computation.3 | convolution fusion | flops 4898914304 | bytes 143785984 | tf_op jit(solution)/shard_map/bqhe,bkhe->bhqk/dot_general | solution.py:19
  281.0 41.0 %fusion = f32[16,2,1024]{2,1,0:T(2,128)S(1)} fusion(f32[16,2,1024,1024]{2,3,1,0:T(8,128)} %get-tuple-element.22, f32[16,2,1024]{2,1,0:T(2,128)S(1)} %get-tuple-element.21), kind=kLoop, calls=%fused_computation.4 | loop fusion | flops 100630528 | bytes 134479872 | tf_op jit(solution)/shard_map/reduce_sum | solution.py:22
  322.0 46.0 %divide_convert_fusion.1 = bf16[16,2,1024,72]{2,3,1,0:T(8,128)(2,1)} fusion(f32[16,2,1024,1024]{2,3,1,0:T(8,128)} %get-tuple-element.22, f32[16,2,1024]{2,1,0:T(2,128)S(1)} %get-tuple-element.21, bf16[16,1024,3,2,72]{1,4,3,0,2:T(8,128)(2,1)} %all_to_all.55, f32[16,2,1024]{2,1,0:T(2,128)S(1)} %fusion), kind=kOutput, calls=%fused_computation.87 | convolution fusion | flops 4937220096 | bytes 143917056 | tf_op jit(solution)/shard_map/bhqk,bkhe->bhqe/dot_general | solution.py:23
  368.0 20.7 %copy.23 = bf16[16,2,1024,72]{3,1,0,2:T(2,128)(2,1)} copy(bf16[16,2,1024,72]{2,3,1,0:T(8,128)(2,1)} %divide_convert_fusion.1) | data formatting | bytes 9437184 | tf_op jit(solution)/shard_map/convert_element_type | solution.py:24
  388.8 6.7 all-to-all-start.1
  398.1 90.9 %all-to-all-done.1 = bf16[16,2,1024,72]{3,1,0,2:T(2,128)(2,1)} async-done(((bf16[16,2,1024,72]{3,1,0,2:T(2,128)(2,1)}), bf16[16,2,1024,72]{3,1,0,2:T(2,128)(2,1)}, u32[]{:S(2)}, u32[]{:S(2)}) %all-to-all-start.1) | async-done | bytes 4718624 | tf_op jit(solution)/shard_map/all_to_all | solution.py:45
  489.0 19.9 %copy.24 = bf16[16,2,8,128,72]{3,4,1,2,0:T(8,128)(2,1)} copy(bf16[16,2,8,128,72]{4,1,0,3,2:T(2,128)(2,1)} %bitcast.10) | data formatting | bytes 9437184 | tf_op jit(solution)/shard_map/all_to_all | solution.py:45
  508.9 11.2 convert_reduce_fusion.2
  520.1 1.4 fusion.54
  521.6 29.9 %fusion.40 = f32[16,128,4304]{1,2,0:T(8,128)} fusion(bf16[2,1152,4304]{1,2,0:T(8,128)(2,1)} %param.22, bf16[16,128,1152]{2,1,0:T(8,128)(2,1)S(1)} %get-tuple-element.24, f32[1152]{0:T(1024)S(1)} %get-tuple-element.12, f32[1152]{0:T(1024)S(1)} %get-tuple-element.33, f32[16,128]{1,0:T(8,128)S(1)} %add_rsqrt_fusion.2, f32[16,128]{1,0:T(8,128)S(1)} %broadcast_multiply_fusion.2), kind=kOutput, calls=%fused_computation.58 | convolution fusion | flops 20322975744 | bytes 49918976 | tf_op jit(solution)/shard_map/bsd,df->bsf/dot_general | solution.py:29
  551.5 34.2 %convert_reduce_fusion.1 = (f32[16,128]{1,0:T(8,128)S(1)}, bf16[16,128,1152]{2,1,0:T(8,128)(2,1)S(1)}) fusion(f32[1152]{0:T(1024)S(1)} %get-tuple-element.8, bf16[2,4304,1152]{2,1,0:T(8,128)(2,1)} %param.24, f32[16,128,4304]{1,2,0:T(8,128)} %fusion.40, f32[4304]{0:T(1024)S(1)} %get-tuple-element.6, bf16[16,128,1152]{2,1,0:T(8,128)(2,1)} %copy-done.2), kind=kOutput, calls=%fused_computation.39 | convolution fusion | flops 20411119616 | bytes 54641984 | tf_op jit(solution)/shard_map/bsf,fd->bsd/dot_general | solution.py:31
  587.8 23.8 %add_convert_fusion = bf16[16,128,3,16,72]{1,4,3,2,0:T(8,128)(2,1)S(1)} fusion(f32[3,16,72]{2,1,0:T(8,128)S(1)} %copy-done.5, bf16[2,1152,3,16,72]{1,4,3,2,0:T(8,128)(2,1)} %param.16, bf16[16,128,1152]{2,1,0:T(8,128)(2,1)} %copy-done.1, f32[1152]{0:T(1024)S(1)} %copy-done.16, f32[1152]{0:T(1024)S(1)} %copy-done.17, f32[16,128]{1,0:T(8,128)S(1)} %add_rsqrt_fusion.1, ...), kind=kOutput, calls=%fused_computation.28 | convolution fusion | flops 16335765504 | bytes 26876416 | tf_op jit(solution)/shard_map/bsd,dthe->bsthe/dot_general | solution.py:42
  611.7 3.7 copy.25
  615.3 159.5 %all_to_all.73 = bf16[16,128,3,16,72]{1,4,2,0,3:T(8,128)(2,1)S(1)} all-to-all(bf16[16,128,3,16,72]{1,4,2,0,3:T(8,128)(2,1)S(1)} %copy.25), channel_id=1, replica_groups=mesh['dp'=4,'sp'=8] {'sp'}, dimensions={3} | all-to-all | bytes 28311552 | tf_op jit(solution)/shard_map/all_to_all | solution.py:43
  774.9 10.7 copy.38
  785.5 21.6 %all_to_all.63 = bf16[16,1024,3,2,72]{1,4,3,0,2:T(8,128)(2,1)} reshape(bf16[16,8,128,3,2,72]{2,1,5,4,0,3:T(8,128)(2,1)} %bitcast.129) | data formatting | bytes 28311552 | tf_op jit(solution)/shard_map/all_to_all | solution.py:43
  807.2 47.3 %multiply_reduce_fusion = (f32[16,2,1024]{2,1,0:T(2,128)S(1)}, f32[16,2,1024,1024]{2,3,1,0:T(8,128)}) fusion(bf16[16,1024,3,2,72]{1,4,3,0,2:T(8,128)(2,1)} %all_to_all.63), kind=kOutput, calls=%fused_computation.2 | convolution fusion | flops 4898914304 | bytes 143785984 | tf_op jit(solution)/shard_map/bqhe,bkhe->bhqk/dot_general | solution.py:19
  854.4 41.0 %fusion.2 = f32[16,2,1024]{2,1,0:T(2,128)S(1)} fusion(f32[16,2,1024,1024]{2,3,1,0:T(8,128)} %get-tuple-element.28, f32[16,2,1024]{2,1,0:T(2,128)S(1)} %get-tuple-element.27), kind=kLoop, calls=%fused_computation.6 | loop fusion | flops 100630528 | bytes 134479872 | tf_op jit(solution)/shard_map/reduce_sum | solution.py:22
  895.4 46.0 %divide_convert_fusion = bf16[16,2,1024,72]{2,3,1,0:T(8,128)(2,1)} fusion(f32[16,2,1024,1024]{2,3,1,0:T(8,128)} %get-tuple-element.28, f32[16,2,1024]{2,1,0:T(2,128)S(1)} %get-tuple-element.27, bf16[16,1024,3,2,72]{1,4,3,0,2:T(8,128)(2,1)} %all_to_all.63, f32[16,2,1024]{2,1,0:T(2,128)S(1)} %fusion.2), kind=kOutput, calls=%fused_computation.86 | convolution fusion | flops 4937220096 | bytes 143917056 | tf_op jit(solution)/shard_map/bhqk,bkhe->bhqe/dot_general | solution.py:23
  941.5 20.7 %copy.28 = bf16[16,2,1024,72]{3,1,0,2:T(2,128)(2,1)} copy(bf16[16,2,1024,72]{2,3,1,0:T(8,128)(2,1)} %divide_convert_fusion) | data formatting | bytes 9437184 | tf_op jit(solution)/shard_map/convert_element_type | solution.py:24
  962.1 100.6 %all_to_all.74 = bf16[16,2,1024,72]{3,1,0,2:T(2,128)(2,1)} all-to-all(bf16[16,2,1024,72]{3,1,0,2:T(2,128)(2,1)} %copy.28), channel_id=1, replica_groups=mesh['dp'=4,'sp'=8] {'sp'}, dimensions={2} | all-to-all | bytes 9437184 | tf_op jit(solution)/shard_map/all_to_all | solution.py:45
  1062.8 19.9 %copy.29 = bf16[16,2,8,128,72]{3,4,1,2,0:T(8,128)(2,1)} copy(bf16[16,2,8,128,72]{4,1,0,3,2:T(2,128)(2,1)} %bitcast.130) | data formatting | bytes 9437184 | tf_op jit(solution)/shard_map/all_to_all | solution.py:45
  1082.7 11.2 convert_reduce_fusion
  1095.4 29.8 %fusion.37 = f32[16,128,4304]{1,2,0:T(8,128)} fusion(bf16[2,1152,4304]{1,2,0:T(8,128)(2,1)} %param.22, bf16[16,128,1152]{2,1,0:T(8,128)(2,1)S(1)} %get-tuple-element.30, f32[1152]{0:T(1024)S(1)} %copy-done.14, f32[1152]{0:T(1024)S(1)} %copy-done.15, f32[16,128]{1,0:T(8,128)S(1)} %add_rsqrt_fusion, f32[16,128]{1,0:T(8,128)S(1)} %broadcast_multiply_fusion), kind=kOutput, calls=%fused_computation.55 | convolution fusion | flops 20322975744 | bytes 49918976 | tf_op jit(solution)/shard_map/bsd,df->bsf/dot_general | solution.py:29
  1125.2 40.4 %fusion.65 = bf16[16,128,1152]{2,1,0:T(8,128)(2,1)} fusion(bf16[16,128,1152]{2,1,0:T(8,128)(2,1)S(1)} %get-tuple-element.30, bf16[2,4304,1152]{2,1,0:T(8,128)(2,1)} %param.24, f32[16,128,4304]{1,2,0:T(8,128)} %fusion.37, f32[4304]{0:T(1024)S(1)} %copy-done.6, f32[1152]{0:T(1024)S(1)} %copy-done.13), kind=kOutput, calls=%fused_computation.83 | convolution fusion | flops 20406403072 | bytes 54633792 | tf_op jit(solution)/shard_map/bsf,fd->bsd/dot_general | solution.py:31
  (54 shorter events, 7.4 us)
Async XLA Ops:
  0.0 8.2 copy-start
  0.0 7.0 copy-start.3
  0.0 7.6 copy-start.7
  0.0 7.6 copy-start.8
  388.8 6.7 copy-start.9
  388.8 7.4 copy-start.10
  388.8 8.0 copy-start.11
  388.8 8.0 copy-start.12
  388.8 8.6 copy-start.4
  388.8 100.2 %all-to-all-start.1 = ((bf16[16,2,1024,72]{3,1,0,2:T(2,128)(2,1)}), bf16[16,2,1024,72]{3,1,0,2:T(2,128)(2,1)}, u32[]{:S(2)}, u32[]{:S(2)}) async-start(bf16[16,2,1024,72]{3,1,0,2:T(2,128)(2,1)} %copy.23), calls=%async_computation.1 | async-start | bytes 16777216 | tf_op jit(solution)/shard_map/all_to_all | solution.py:45
  520.1 31.4 %copy-start.2 = (bf16[16,128,1152]{2,1,0:T(8,128)(2,1)}, bf16[16,128,1152]{2,1,0:T(8,128)(2,1)S(1)}, u32[]{:S(2)}) copy-start(bf16[16,128,1152]{2,1,0:T(8,128)(2,1)S(1)} %get-tuple-element.24) | copy-start | bytes 14155780
  551.5 36.4 %copy-start.5 = (f32[3,16,72]{2,1,0:T(8,128)S(1)}, f32[3,16,72]{2,1,0:T(8,128)}, u32[]{:S(2)}) copy-start(f32[3,16,72]{2,1,0:T(8,128)} %get-tuple-element.19) | copy-start | bytes 41476
  551.5 36.4 %copy-start.16 = (f32[1152]{0:T(1024)S(1)}, f32[1152]{0:T(1024)}, u32[]{:S(2)}) copy-start(f32[1152]{0:T(1024)} %get-tuple-element.17) | copy-start | bytes 13828
  551.5 36.4 %copy-start.17 = (f32[1152]{0:T(1024)S(1)}, f32[1152]{0:T(1024)}, u32[]{:S(2)}) copy-start(f32[1152]{0:T(1024)} %get-tuple-element.32) | copy-start | bytes 13828
  585.6 2.2 copy-start.1
  1062.8 19.9 %copy-start.18 = (f32[1152]{0:T(1024)S(1)}, f32[1152]{0:T(1024)}, u32[]{:S(2)}) copy-start(f32[1152]{0:T(1024)} %get-tuple-element.13) | copy-start | bytes 13828
  1082.7 12.7 %copy-start.14 = (f32[1152]{0:T(1024)S(1)}, f32[1152]{0:T(1024)}, u32[]{:S(2)}) copy-start(f32[1152]{0:T(1024)} %get-tuple-element.11) | copy-start | bytes 13828
  1082.7 12.7 %copy-start.15 = (f32[1152]{0:T(1024)S(1)}, f32[1152]{0:T(1024)}, u32[]{:S(2)}) copy-start(f32[1152]{0:T(1024)} %get-tuple-element.34) | copy-start | bytes 13828
  1095.4 29.8 %copy-start.6 = (f32[4304]{0:T(1024)S(1)}, f32[4304]{0:T(1024)}, u32[]{:S(2)}) copy-start(f32[4304]{0:T(1024)} %get-tuple-element.5) | copy-start | bytes 51652
  1095.4 29.8 %copy-start.13 = (f32[1152]{0:T(1024)S(1)}, f32[1152]{0:T(1024)}, u32[]{:S(2)}) copy-start(f32[1152]{0:T(1024)} %get-tuple-element.7) | copy-start | bytes 13828
where the time goes:
time: 1170 us
  blocking collectives  422 us (36%)
  matrix products  392 us (34%)
  local copies, waits for them, and re-layouts  161 us (14%)
  other arithmetic  93.2 us (8%)
  waiting for transfers between devices  90.9 us (8%)
    all_to_all x2, blocking collectives, device_step(): qkv_heads = lax.all_to_all(qkv_local, 'sp', 3, 1, tiled=True)  321 us
    all_to_all x1, blocking collectives, device_step(): attn_tokens = lax.all_to_all(attn_heads, 'sp', 2, 1, tiled=True)  101 us
    dot_general x2, matrix products, attend(): jnp.einsum('bqhe,bkhe->bhqk', q_part, k_part, preferred_element_type=jnp....  94.5 us
    dot_general x2, matrix products, attend(): jnp.einsum('bhqk,bkhe->bhqe', prob_vals.astype(jnp.bfloat16), v_part, pre...  92.1 us
    all_to_all x1, waiting for transfers between devices, device_step(): attn_tokens = lax.all_to_all(attn_heads, 'sp', 2, 1, tiled=True)  90.9 us
    reduce_sum x2, other arithmetic, attend(): row_total = jnp.sum(prob_vals, axis=-1, keepdims=True)  82 us
    dot_general x2, matrix products, mlp_block(): jnp.einsum('bsf,fd->bsd', active, w_down, preferred_element_type=jnp.floa...  74.6 us
    all_to_all x4, local copies, waits for them, and re-layouts, device_step(): qkv_heads = lax.all_to_all(qkv_local, 'sp', 3, 1, tiled=True)  64.6 us
  transfers between devices with their start and end apart: 1, of which 1 were waited for; matrix products, arithmetic and copies ran while one was open for 0% of the time, Pallas kernels for 0%

commit v1 on v0

v1 whole, which is shorter than its diff:
```python
import functools
import math

import jax
import jax.numpy as jnp
from jax import lax
from jax.experimental import pallas as pl
from jax.experimental.pallas import tpu as pltpu
from jax.sharding import PartitionSpec as P

LN_EPS = 1e-6
BF16 = jnp.bfloat16
F32 = jnp.float32
NT = (((1,), (1,)), ((), ()))
VMEM_LIMIT = 60 << 20
WINDOW = 256


def layer_norm(values, gain, shift):
    values = values.astype(F32)
    centred = values - jnp.mean(values, axis=-1, keepdims=True)
    var = jnp.mean(centred * centred, axis=-1, keepdims=True)
    return (centred * lax.rsqrt(var + LN_EPS) * gain + shift).astype(BF16)


def whole(shape):
    return pl.BlockSpec(shape, lambda i: (0,) * len(shape), pipeline_mode=pl.Buffered(1))


def layer_of(layer, shape):
    return pl.BlockSpec((None,) + shape, lambda i: (layer,) + (0,) * len(shape), pipeline_mode=pl.Buffered(1))


def qkv_kernel(x_ref, gain_ref, shift_ref, w_ref, bias_ref, out_ref, *, layer, cols):
    row = slice(layer, layer + 1)
    normed = layer_norm(x_ref[...], gain_ref[row, :], shift_ref[row, :])
    n_out = w_ref.shape[0]
    for c in range(0, n_out, cols):
        w = min(cols, n_out - c)
        y = lax.dot_general(normed, w_ref[c:c + w, :], NT, preferred_element_type=F32)
        out_ref[:, c:c + w] = (y + bias_ref[row, c:c + w]).astype(BF16)


def qkv_call(layer, x, gain, shift, w, bias, rows=512, cols=256):
    m, d = x.shape
    n = w.shape[1]
    return pl.pallas_call(
        functools.partial(qkv_kernel, layer=layer, cols=cols),
        grid=(m // rows,),
        name="qkv",
        in_specs=[pl.BlockSpec((rows, d), lambda i: (i, 0)), whole(gain.shape), whole(shift.shape), layer_of(layer, (n, d)), whole(bias.shape)],
        out_specs=pl.BlockSpec((rows, n), lambda i: (i, 0)),
        out_shape=jax.ShapeDtypeStruct((m, n), BF16),
        compiler_params=pltpu.CompilerParams(vmem_limit_bytes=VMEM_LIMIT),
        cost_estimate=pl.CostEstimate(flops=2 * m * d * n, bytes_accessed=2 * (m * d + n * d + m * n), transcendentals=0),
    )(x, gain, shift, w, bias)


def attn_kernel(qkv_ref, out_ref, s0_ref, s1_ref, k0_ref, k1_ref, *, heads, head_dim, rows, unroll):
    seq = qkv_ref.shape[0]
    d = heads * head_dim
    blocks = seq // rows
    score_scale = (head_dim ** -0.5) * math.log2(math.e)
    s_bufs, k_bufs = (s0_ref, s1_ref), (k0_ref, k1_ref)

    def window(h):
        low = h * head_dim
        off = pl.multiple_of(jnp.minimum(low // 128, d // 128 - 2) * 128, 128)
        low = low - off
        lane = lax.broadcasted_iota(jnp.int32, (1, WINDOW), 1)
        return off, (lane >= low) & (lane < low + head_dim)

    def mask_keys(h, k_buf):
        off, mask = window(h)
        k = qkv_ref[:, pl.ds(pl.multiple_of(d + off, 128), WINDOW)]
        k_buf[...] = jnp.where(mask, k, jnp.zeros_like(k))

    def scores(h, j, s_buf, k_buf):
        off, _ = window(h)
        q = qkv_ref[j * rows:(j + 1) * rows, pl.ds(off, WINDOW)]
        s_buf[...] = lax.dot_general(q, k_buf[...], NT, preferred_element_type=F32)

    mask_keys(0, k_bufs[0])
    scores(0, 0, s_bufs[0], k_bufs[0])

    def some_heads(i, carry):
        t = 0
        for u in range(unroll):
            h = i * unroll + u
            off, mask = window(h)
            for j in range(blocks):
                if j + 1 < blocks:
                    scores(h, j + 1, s_bufs[(t + 1) % 2], k_bufs[u % 2])
                else:
                    after = jnp.minimum(h + 1, heads - 1)
                    mask_keys(after, k_bufs[(u + 1) % 2])
                    scores(after, 0, s_bufs[(t + 1) % 2], k_bufs[(u + 1) % 2])
                s = s_bufs[t % 2][...]
                peak = jnp.max(s, axis=-1, keepdims=True)
                p = jnp.exp2((s - peak) * score_scale)
                total = jnp.sum(p, axis=-1, keepdims=True)
                v = qkv_ref[:, pl.ds(pl.multiple_of(2 * d + off, 128), WINDOW)]
                o = jnp.dot(p.astype(BF16), v, preferred_element_type=F32)
                o = (o * (1.0 / total)).astype(BF16)
                place = (pl.ds(j * rows, rows), pl.ds(off, WINDOW))
                out_ref[place] = jnp.where(mask, o, out_ref[place])
                t += 1
        return carry

    lax.fori_loop(0, heads // unroll, some_heads, 0)


def attn_call(qkv, images, heads, head_dim, rows=512, unroll=2):
    m, n = qkv.shape
    seq = m // images
    d = heads * head_dim
    return pl.pallas_call(
        functools.partial(attn_kernel, heads=heads, head_dim=head_dim, rows=rows, unroll=unroll),
        grid=(images,),
        name="attn",
        in_specs=[pl.BlockSpec((seq, n), lambda i: (i, 0))],
        out_specs=pl.BlockSpec((seq, d), lambda i: (i, 0)),
        out_shape=jax.ShapeDtypeStruct((m, d), BF16),
        scratch_shapes=[pltpu.VMEM((rows, seq), F32)] * 2 + [pltpu.VMEM((seq, WINDOW), BF16)] * 2,
        compiler_params=pltpu.CompilerParams(vmem_limit_bytes=VMEM_LIMIT),
        cost_estimate=pl.CostEstimate(flops=8 * images * heads * seq * seq * 256, bytes_accessed=2 * (m * n + m * d), transcendentals=images * heads * seq * seq),
    )(qkv)


def proj_kernel(o_ref, h_ref, wo_ref, bo_ref, out_ref, *, layer):
    proj = jnp.dot(o_ref[...], wo_ref[...], preferred_element_type=F32) + bo_ref[layer:layer + 1, :]
    out_ref[...] = (h_ref[...].astype(F32) + proj).astype(BF16)


def proj_call(layer, o, h, wo, bo, rows=512):
    m, d = o.shape
    block = pl.BlockSpec((rows, d), lambda i: (i, 0))
    return pl.pallas_call(
        functools.partial(proj_kernel, layer=layer),
        grid=(m // rows,),
        name="proj",
        in_specs=[block, block, layer_of(layer, (d, d)), whole(bo.shape)],
        out_specs=block,
        out_shape=jax.ShapeDtypeStruct((m, d), BF16),
        compiler_params=pltpu.CompilerParams(vmem_limit_bytes=VMEM_LIMIT),
        cost_estimate=pl.CostEstimate(flops=2 * m * d * d, bytes_accessed=2 * (3 * m * d + d * d), transcendentals=0),
    )(o, h, wo, bo)


def mlp_kernel(*refs, layer, cols):
    mid_ref, gain_ref, shift_ref, wu_ref, bu_ref, wd_ref, bd_ref = refs[:7]
    out_ref, act_ref = refs[-2:]
    row = slice(layer, layer + 1)
    f = wu_ref.shape[0]
    normed = layer_norm(mid_ref[...], gain_ref[row, :], shift_ref[row, :])
    for c in range(0, f, cols):
        w = min(cols, f - c)
        up = lax.dot_general(normed, wu_ref[c:c + w, :], NT, preferred_element_type=F32) + bu_ref[row, c:c + w]
        act_ref[:, c:c + w] = jax.nn.gelu(up, approximate=True).astype(BF16)
    down = jnp.dot(act_ref[...], wd_ref[...], preferred_element_type=F32) + bd_ref[row, :]
    out_ref[...] = (mid_ref[...].astype(F32) + down).astype(BF16)


def mlp_call(layer, mid, gain, shift, wu, bu, wd, bd, rows=256, cols=512, total=None, start=0, into=None):
    m, d = mid.shape
    f = wu.shape[1]
    total = m if total is None else total
    first = start // rows
    args = [mid, gain, shift, wu, bu, wd, bd]
    specs = [pl.BlockSpec((rows, d), lambda i: (i, 0)), whole(gain.shape), whole(shift.shape), layer_of(layer, (f, d)), whole(bu.shape), layer_of(layer, (f, d)), whole(bd.shape)]
    if into is not None:
        args.append(into)
        specs.append(pl.BlockSpec(memory_space=pl.ANY))
    return pl.pallas_call(
        functools.partial(mlp_kernel, layer=layer, cols=cols),
        grid=(m // rows,),
        name="mlp",
        in_specs=specs,
        out_specs=pl.BlockSpec((rows, d), lambda i: (first + i, 0)),
        out_shape=jax.ShapeDtypeStruct((total, d), BF16),
        scratch_shapes=[pltpu.VMEM((rows, f), BF16)],
        input_output_aliases={7: 0} if into is not None else {},
        compiler_params=pltpu.CompilerParams(vmem_limit_bytes=VMEM_LIMIT),
        cost_estimate=pl.CostEstimate(flops=4 * m * d * f, bytes_accessed=4 * (m * d + f * d), transcendentals=m * f),
    )(*args)


def solution(mesh):
    token_spec = P('dp', 'sp', None)
    group = mesh.shape['sp']

    def device_step(image_tokens, ln1_gain, ln1_shift, w_qkv, b_qkv, w_out, b_out, ln2_gain, ln2_shift, w_up, b_up, w_down, b_down):
        images, tokens, d = image_tokens.shape
        layers, _, _, heads, head_dim = w_qkv.shape
        w_qkv_t = jnp.transpose(w_qkv, (0, 2, 3, 4, 1)).reshape(layers, 3 * d, d)
        w_up_t = jnp.transpose(w_up, (0, 2, 1))
        w_o = w_out.reshape(layers, d, d)
        b_in = b_qkv.reshape(layers, 3 * d)
        rounds = images // group
        part = group * tokens

        def exchange(rows):
            blocks = rows.reshape(group, tokens, rows.shape[-1])
            return lax.all_to_all(blocks, 'sp', 0, 0, tiled=True).reshape(part, rows.shape[-1])

        def qkv(l, h):
            return qkv_call(l, h, ln1_gain, ln1_shift, w_qkv_t, b_in)

        def mlp(l, mid, **kw):
            return mlp_call(l, mid, ln2_gain, ln2_shift, w_up_t, b_up, w_down, b_down, **kw)

        own = image_tokens.reshape(rounds, part, d)
        mids = []
        for r in range(rounds):
            h = exchange(own[r])
            x = qkv(0, h) if r == 0 else exchange(qkv(0, own[r]))
            for l in range(layers):
                if l:
                    x = qkv(l, h)
                o = attn_call(x, 1, heads, head_dim)
                mid = proj_call(l, o, h, w_o, b_out)
                if l < layers - 1:
                    h = mlp(l, mid)
            mids.append(exchange(mid))
        out = None
        for r in range(rounds):
            out = mlp(layers - 1, mids[r], total=rounds * part, start=r * part, into=out)
        return out.reshape(images, tokens, d)

    return jax.shard_map(device_step, mesh=mesh, in_specs=(token_spec,) + (P(),) * 12, out_specs=token_spec, check_vma=False)
```

time: 1170 us -> 407 us (0.35)
  blocking collectives: 422 us -> 0 us
  matrix products: 392 us -> 0 us
  Pallas kernels: 0 us -> 352 us
  local copies, waits for them, and re-layouts: 161 us -> 10 us
  other arithmetic: 93.2 us -> 0 us
  waiting for transfers between devices: 90.9 us -> 11.8 us
  starting transfers between devices: 6.71 us -> 27.2 us
    all_to_all x3 -> x0, blocking collectives: 422 us -> none  [the longest x2 321 us: device_step(): qkv_heads = lax.all_to_all(qkv_local, 'sp', 3, 1, tiled=True)]
    dot_general x12 -> x0, matrix products: 392 us -> none  [the longest x2 94.5 us: attend(): jnp.einsum('bqhe,bkhe->bhqk', q_part, k_part, preferred_element_type=jnp....]
    pallas_call x0 -> x16, Pallas kernels: none -> 352 us  [the longest x4 137 us: mlp_call(): pl.pallas_call(functools.partial(mlp_kernel, layer=layer, cols=cols), gri...]
    all_to_all x6 -> x0, local copies, waits for them, and re-layouts: 104 us -> none  [the longest x4 64.6 us: device_step(): qkv_heads = lax.all_to_all(qkv_local, 'sp', 3, 1, tiled=True)]
    reduce_sum x7 -> x0, other arithmetic: 93.1 us -> none  [the longest x2 82 us: attend(): row_total = jnp.sum(prob_vals, axis=-1, keepdims=True)]
    all_to_all x1 -> x5, waiting for transfers between devices: 90.9 us -> 11.8 us  [exchange(): lax.all_to_all(blocks, 'sp', 0, 0, tiled=True).reshape(part, rows.shape[-1])]
    convert_element_type x4 -> x0, local copies, waits for them, and re-layouts: 51.7 us -> none  [the longest x2 41.4 us: attend(): return (mixed_vals / row_total).astype(jnp.bfloat16)]
    all_to_all x1 -> x5, starting transfers between devices: 6.71 us -> 27.2 us  [exchange(): lax.all_to_all(blocks, 'sp', 0, 0, tiled=True).reshape(part, rows.shape[-1])]
  transfers between devices with their start and end apart: 1 -> 5, of which waited for: 1 -> 1; matrix products, arithmetic and copies ran while one was open for 0% -> 0% of each run, Pallas kernels for 0% -> 79%
where the time goes in v1:
time: 407 us; the launch traced here: 401 us
  Pallas kernels  352 us (86%)
  starting transfers between devices  27.2 us (7%)
  waiting for transfers between devices  11.8 us (3%)
  local copies, waits for them, and re-layouts  10 us (2%)
    pallas_call x4, Pallas kernels, mlp_call(): pl.pallas_call(functools.partial(mlp_kernel, layer=layer, cols=cols), gri...  137 us
    pallas_call x4, Pallas kernels, attn_call(): pl.pallas_call(functools.partial(attn_kernel, heads=heads, head_dim=head_...  121 us
    pallas_call x4, Pallas kernels, qkv_call(): pl.pallas_call(functools.partial(qkv_kernel, layer=layer, cols=cols), gri...  65.3 us
    pallas_call x4, Pallas kernels, proj_call(): pl.pallas_call(functools.partial(proj_kernel, layer=layer), grid=(m // ro...  28.9 us
    all_to_all x5, starting transfers between devices, exchange(): lax.all_to_all(blocks, 'sp', 0, 0, tiled=True).reshape(part, rows.shape[-1])  27.2 us
    all_to_all x5, waiting for transfers between devices, exchange(): lax.all_to_all(blocks, 'sp', 0, 0, tiled=True).reshape(part, rows.shape[-1])  11.8 us
  transfers between devices with their start and end apart: 5, of which 1 were waited for; matrix products, arithmetic and copies ran while one was open for 0% of the time, Pallas kernels for 79%

profile of v1, /device:TPU:81, one launch (start us, length us, event | category | flops | bytes accessed | tf_op | source)
XLA Modules:
  0.0 401.5 jit_solution(5871786065776811559)
XLA Ops:
  0.0 5.1 %fusion = (bf16[8,128,1152]{2,1,0:T(8,128)(2,1)}, bf16[8,128,1152]{2,1,0:T(8,128)(2,1)}) fusion(bf16[16,128,1152]{2,1,0:T(8,128)(2,1)} %param.13), kind=kLoop, calls=%fused_computation | loop fusion | bytes 9437184 | tf_op jit(solution)/shard_map/slice | solution.py:215
  5.1 6.1 %all-to-all-start.3 = ((bf16[8,128,1152]{2,1,0:T(8,128)(2,1)}), bf16[8,128,1152]{2,1,0:T(8,128)(2,1)S(1)}, u32[]{:S(2)}, u32[]{:S(2)}) async-start(bf16[8,128,1152]{2,1,0:T(8,128)(2,1)} %get-tuple-element.5), calls=%async_computation.3 | async-start | bytes 4718592 | tf_op jit(solution)/shard_map/all_to_all | solution.py:204
  11.2 0.0 copy-done.3
  11.3 0.7 reshape.43.bias_ref
  12.0 16.3 %qkv.4 = bf16[1024,3456]{1,0:T(8,128)(2,1)} custom-call(bf16[1024,1152]{1,0:T(8,128)(2,1)} %bitcast.x_ref, f32[2,1152]{1,0:T(2,128)} %gain_ref.7, f32[2,1152]{1,0:T(2,128)} %shift_ref.7, bf16[2,3456,1152]{2,1,0:T(8,128)(2,1)} %bitcast.31, f32[2,3456]{1,0:T(2,128)} %reshape.43.bias_ref), custom_call_target="tpu_custom_call" | custom-call | flops 8153726976 | bytes 17399808 | tf_op jit(solution)/shard_map/qkv/pallas_call | solution.py:47
  28.3 11.7 %all-to-all-done.3 = bf16[8,128,1152]{2,1,0:T(8,128)(2,1)S(1)} async-done(((bf16[8,128,1152]{2,1,0:T(8,128)(2,1)}), bf16[8,128,1152]{2,1,0:T(8,128)(2,1)S(1)}, u32[]{:S(2)}, u32[]{:S(2)}) %all-to-all-start.3) | async-done | bytes 2359328 | tf_op jit(solution)/shard_map/all_to_all | solution.py:204
  40.1 1.4 copy-done
  41.5 6.2 %all-to-all-start = ((bf16[8,128,3456]{2,1,0:T(8,128)(2,1)}), bf16[8,128,3456]{2,1,0:T(8,128)(2,1)}, u32[]{:S(2)}, u32[]{:S(2)}) async-start(bf16[8,128,3456]{2,1,0:T(8,128)(2,1)} %bitcast.25), calls=%async_computation | async-start | bytes 14155776 | tf_op jit(solution)/shard_map/all_to_all | solution.py:204
  47.7 16.3 %qkv.6.qkv_ref = bf16[1024,3456]{1,0:T(8,128)(2,1)} custom-call(bf16[1024,1152]{1,0:T(8,128)(2,1)} %bitcast.21, f32[2,1152]{1,0:T(2,128)} %gain_ref.7, f32[2,1152]{1,0:T(2,128)} %shift_ref.7, bf16[2,3456,1152]{2,1,0:T(8,128)(2,1)} %bitcast.32, f32[2,3456]{1,0:T(2,128)} %reshape.43.bias_ref), custom_call_target="tpu_custom_call" | custom-call | flops 8153726976 | bytes 17399808 | tf_op jit(solution)/shard_map/qkv/pallas_call | solution.py:47
  63.9 30.2 %attn.6.o_ref = bf16[1024,1152]{1,0:T(8,128)(2,1)} custom-call(bf16[1024,3456]{1,0:T(8,128)(2,1)} %qkv.6.qkv_ref), custom_call_target="tpu_custom_call" | custom-call | flops 34359738368 | bytes 9437184 | tf_op jit(solution)/shard_map/attn/pallas_call | solution.py:117
  94.2 7.2 %proj.6.refs_0_ = bf16[1024,1152]{1,0:T(8,128)(2,1)} custom-call(bf16[1024,1152]{1,0:T(8,128)(2,1)} %attn.6.o_ref, bf16[1024,1152]{1,0:T(8,128)(2,1)} %bitcast.22, bf16[2,1152,1152]{2,1,0:T(8,128)(2,1)} %bitcast.17, f32[2,1152]{1,0:T(2,128)} %bo_ref.7), custom_call_target="tpu_custom_call" | custom-call | flops 2717908992 | bytes 9732096 | tf_op jit(solution)/shard_map/proj/pallas_call | solution.py:138
  101.4 34.4 %mlp.5.x_ref.h_ref = bf16[1024,1152]{1,0:T(8,128)(2,1)} custom-call(bf16[1024,1152]{1,0:T(8,128)(2,1)} %proj.6.refs_0_, f32[2,1152]{1,0:T(2,128)} %refs_1_.7, f32[2,1152]{1,0:T(2,128)} %refs_2_.7, bf16[2,4304,1152]{2,1,0:T(8,128)(2,1)} %bitcast.27, f32[2,4304]{1,0:T(2,128)} %refs_4_.7, bf16[2,4304,1152]{2,1,0:T(8,128)(2,1)} %refs_5_.7, f32[2,1152]{1,0:T(2,128)} %refs_6_.7), custom_call_target="tpu_custom_call" | custom-call | flops 20308819968 | bytes 24551424 | tf_op jit(solution)/shard_map/mlp/pallas_call | solution.py:174
  135.8 16.2 %qkv.7.qkv_ref = bf16[1024,3456]{1,0:T(8,128)(2,1)} custom-call(bf16[1024,1152]{1,0:T(8,128)(2,1)} %mlp.5.x_ref.h_ref, f32[2,1152]{1,0:T(2,128)} %gain_ref.7, f32[2,1152]{1,0:T(2,128)} %shift_ref.7, bf16[2,3456,1152]{2,1,0:T(8,128)(2,1)} %bitcast.33, f32[2,3456]{1,0:T(2,128)} %reshape.43.bias_ref), custom_call_target="tpu_custom_call" | custom-call | flops 8153726976 | bytes 17399808 | tf_op jit(solution)/shard_map/qkv/pallas_call | solution.py:47
  152.0 30.6 %attn.7.o_ref = bf16[1024,1152]{1,0:T(8,128)(2,1)} custom-call(bf16[1024,3456]{1,0:T(8,128)(2,1)} %qkv.7.qkv_ref), custom_call_target="tpu_custom_call" | custom-call | flops 34359738368 | bytes 9437184 | tf_op jit(solution)/shard_map/attn/pallas_call | solution.py:117
  182.6 7.2 %proj.7 = bf16[1024,1152]{1,0:T(8,128)(2,1)} custom-call(bf16[1024,1152]{1,0:T(8,128)(2,1)} %attn.7.o_ref, bf16[1024,1152]{1,0:T(8,128)(2,1)} %mlp.5.x_ref.h_ref, bf16[2,1152,1152]{2,1,0:T(8,128)(2,1)} %bitcast.18, f32[2,1152]{1,0:T(2,128)} %bo_ref.7), custom_call_target="tpu_custom_call" | custom-call | flops 2717908992 | bytes 9732096 | tf_op jit(solution)/shard_map/proj/pallas_call | solution.py:138
  189.9 0.0 all-to-all-done
  189.9 4.9 %all-to-all-start.1 = ((bf16[8,128,1152]{2,1,0:T(8,128)(2,1)}), bf16[8,128,1152]{2,1,0:T(8,128)(2,1)S(1)}, u32[]{:S(2)}, u32[]{:S(2)}) async-start(bf16[8,128,1152]{2,1,0:T(8,128)(2,1)} %get-tuple-element.6), calls=%async_computation.1 | async-start | bytes 4718592 | tf_op jit(solution)/shard_map/all_to_all | solution.py:204
  194.8 30.2 %attn.4.o_ref = bf16[1024,1152]{1,0:T(8,128)(2,1)} custom-call(bf16[1024,3456]{1,0:T(8,128)(2,1)} %bitcast.4.qkv_ref), custom_call_target="tpu_custom_call" | custom-call | flops 34359738368 | bytes 9437184 | tf_op jit(solution)/shard_map/attn/pallas_call | solution.py:117
  224.9 0.0 all-to-all-done.1
  224.9 1.4 copy-done.1
  226.3 5.1 %all-to-all-start.4 = ((bf16[8,128,1152]{2,1,0:T(8,128)(2,1)}), bf16[8,128,1152]{2,1,0:T(8,128)(2,1)}, u32[]{:S(2)}, u32[]{:S(2)}) async-start(bf16[8,128,1152]{2,1,0:T(8,128)(2,1)} %bitcast.12), calls=%async_computation.4 | async-start | bytes 4718592 | tf_op jit(solution)/shard_map/all_to_all | solution.py:204
  231.5 7.2 %proj.4.refs_0_ = bf16[1024,1152]{1,0:T(8,128)(2,1)} custom-call(bf16[1024,1152]{1,0:T(8,128)(2,1)} %attn.4.o_ref, bf16[1024,1152]{1,0:T(8,128)(2,1)} %bitcast.23, bf16[2,1152,1152]{2,1,0:T(8,128)(2,1)} %bitcast.19, f32[2,1152]{1,0:T(2,128)} %bo_ref.7), custom_call_target="tpu_custom_call" | custom-call | flops 2717908992 | bytes 9732096 | tf_op jit(solution)/shard_map/proj/pallas_call | solution.py:138
  238.7 34.1 %mlp.4.x_ref.h_ref = bf16[1024,1152]{1,0:T(8,128)(2,1)} custom-call(bf16[1024,1152]{1,0:T(8,128)(2,1)} %proj.4.refs_0_, f32[2,1152]{1,0:T(2,128)} %refs_1_.7, f32[2,1152]{1,0:T(2,128)} %refs_2_.7, bf16[2,4304,1152]{2,1,0:T(8,128)(2,1)} %bitcast.28, f32[2,4304]{1,0:T(2,128)} %refs_4_.7, bf16[2,4304,1152]{2,1,0:T(8,128)(2,1)} %refs_5_.7, f32[2,1152]{1,0:T(2,128)} %refs_6_.7), custom_call_target="tpu_custom_call" | custom-call | flops 20308819968 | bytes 24551424 | tf_op jit(solution)/shard_map/mlp/pallas_call | solution.py:174
  272.8 16.5 %qkv.5.qkv_ref = bf16[1024,3456]{1,0:T(8,128)(2,1)} custom-call(bf16[1024,1152]{1,0:T(8,128)(2,1)} %mlp.4.x_ref.h_ref, f32[2,1152]{1,0:T(2,128)} %gain_ref.7, f32[2,1152]{1,0:T(2,128)} %shift_ref.7, bf16[2,3456,1152]{2,1,0:T(8,128)(2,1)} %bitcast.34, f32[2,3456]{1,0:T(2,128)} %reshape.43.bias_ref), custom_call_target="tpu_custom_call" | custom-call | flops 8153726976 | bytes 17399808 | tf_op jit(solution)/shard_map/qkv/pallas_call | solution.py:47
  289.3 30.2 %attn.5.o_ref = bf16[1024,1152]{1,0:T(8,128)(2,1)} custom-call(bf16[1024,3456]{1,0:T(8,128)(2,1)} %qkv.5.qkv_ref), custom_call_target="tpu_custom_call" | custom-call | flops 34359738368 | bytes 9437184 | tf_op jit(solution)/shard_map/attn/pallas_call | solution.py:117
  319.6 7.2 %proj.5 = bf16[1024,1152]{1,0:T(8,128)(2,1)} custom-call(bf16[1024,1152]{1,0:T(8,128)(2,1)} %attn.5.o_ref, bf16[1024,1152]{1,0:T(8,128)(2,1)} %mlp.4.x_ref.h_ref, bf16[2,1152,1152]{2,1,0:T(8,128)(2,1)} %bitcast.20, f32[2,1152]{1,0:T(2,128)} %bo_ref.7), custom_call_target="tpu_custom_call" | custom-call | flops 2717908992 | bytes 9732096 | tf_op jit(solution)/shard_map/proj/pallas_call | solution.py:138
  326.7 0.0 all-to-all-done.4
  326.8 4.8 %all-to-all-start.2 = ((bf16[8,128,1152]{2,1,0:T(8,128)(2,1)}), bf16[8,128,1152]{2,1,0:T(8,128)(2,1)S(1)}, u32[]{:S(2)}, u32[]{:S(2)}) async-start(bf16[8,128,1152]{2,1,0:T(8,128)(2,1)} %bitcast.24), calls=%async_computation.2 | async-start | bytes 4718592 | tf_op jit(solution)/shard_map/all_to_all | solution.py:204
  331.6 34.1 %mlp.6.refs_7_ = bf16[2048,1152]{1,0:T(8,128)(2,1)} custom-call(bf16[1024,1152]{1,0:T(8,128)(2,1)} %bitcast.13.refs_0_, f32[2,1152]{1,0:T(2,128)} %refs_1_.7, f32[2,1152]{1,0:T(2,128)} %refs_2_.7, bf16[2,4304,1152]{2,1,0:T(8,128)(2,1)} %bitcast.29, f32[2,4304]{1,0:T(2,128)} %refs_4_.7, bf16[2,4304,1152]{2,1,0:T(8,128)(2,1)} %refs_5_.7, f32[2,1152]{1,0:T(2,128)} %refs_6_.7), custom_call_target="tpu_custom_call" | custom-call | flops 20308819968 | bytes 24551424 | tf_op jit(solution)/shard_map/mlp/pallas_call | solution.py:174
  365.7 0.0 all-to-all-done.2
  365.7 1.4 copy-done.2
  367.1 34.1 %mlp.7 = bf16[2048,1152]{1,0:T(8,128)(2,1)} custom-call(bf16[1024,1152]{1,0:T(8,128)(2,1)} %bitcast.26, f32[2,1152]{1,0:T(2,128)} %refs_1_.7, f32[2,1152]{1,0:T(2,128)} %refs_2_.7, bf16[2,4304,1152]{2,1,0:T(8,128)(2,1)} %bitcast.30, f32[2,4304]{1,0:T(2,128)} %refs_4_.7, bf16[2,4304,1152]{2,1,0:T(8,128)(2,1)} %refs_5_.7, ...), custom_call_target="tpu_custom_call", output_to_operand_aliasing={{}: (7, {})} | custom-call | flops 20308819968 | bytes 24551424 | tf_op jit(solution)/shard_map/mlp/pallas_call | solution.py:174
  (4 shorter events, 0.0 us)
Async XLA Ops:
  5.1 6.2 %copy-start.3 = (f32[2,3,16,72]{3,2,1,0:T(8,128)S(1)}, f32[2,3,16,72]{3,2,1,0:T(8,128)}, u32[]{:S(2)}) copy-start(f32[2,3,16,72]{3,2,1,0:T(8,128)} %param.17) | copy-start | bytes 82948
  5.1 35.0 %all-to-all-start.3 = ((bf16[8,128,1152]{2,1,0:T(8,128)(2,1)}), bf16[8,128,1152]{2,1,0:T(8,128)(2,1)S(1)}, u32[]{:S(2)}, u32[]{:S(2)}) async-start(bf16[8,128,1152]{2,1,0:T(8,128)(2,1)} %get-tuple-element.5), calls=%async_computation.3 | async-start | bytes 4718592 | tf_op jit(solution)/shard_map/all_to_all | solution.py:204
  40.1 1.4 copy-start
  41.5 148.4 %all-to-all-start = ((bf16[8,128,3456]{2,1,0:T(8,128)(2,1)}), bf16[8,128,3456]{2,1,0:T(8,128)(2,1)}, u32[]{:S(2)}, u32[]{:S(2)}) async-start(bf16[8,128,3456]{2,1,0:T(8,128)(2,1)} %bitcast.25), calls=%async_computation | async-start | bytes 14155776 | tf_op jit(solution)/shard_map/all_to_all | solution.py:204
  189.9 35.1 %all-to-all-start.1 = ((bf16[8,128,1152]{2,1,0:T(8,128)(2,1)}), bf16[8,128,1152]{2,1,0:T(8,128)(2,1)S(1)}, u32[]{:S(2)}, u32[]{:S(2)}) async-start(bf16[8,128,1152]{2,1,0:T(8,128)(2,1)} %get-tuple-element.6), calls=%async_computation.1 | async-start | bytes 4718592 | tf_op jit(solution)/shard_map/all_to_all | solution.py:204
  224.9 1.4 copy-start.1
  226.3 100.4 %all-to-all-start.4 = ((bf16[8,128,1152]{2,1,0:T(8,128)(2,1)}), bf16[8,128,1152]{2,1,0:T(8,128)(2,1)}, u32[]{:S(2)}, u32[]{:S(2)}) async-start(bf16[8,128,1152]{2,1,0:T(8,128)(2,1)} %bitcast.12), calls=%async_computation.4 | async-start | bytes 4718592 | tf_op jit(solution)/shard_map/all_to_all | solution.py:204
  326.8 38.9 %all-to-all-start.2 = ((bf16[8,128,1152]{2,1,0:T(8,128)(2,1)}), bf16[8,128,1152]{2,1,0:T(8,128)(2,1)S(1)}, u32[]{:S(2)}, u32[]{:S(2)}) async-start(bf16[8,128,1152]{2,1,0:T(8,128)(2,1)} %bitcast.24), calls=%async_computation.2 | async-start | bytes 4718592 | tf_op jit(solution)/shard_map/all_to_all | solution.py:204
  365.7 1.4 copy-start.2

commit v2 on v1

v2 whole, which is shorter than its diff:
```python
import functools
import math

import jax
import jax.numpy as jnp
from jax import lax
from jax.experimental import pallas as pl
from jax.experimental.pallas import tpu as pltpu
from jax.sharding import PartitionSpec as P

LN_EPS = 1e-6
BF16 = jnp.bfloat16
F32 = jnp.float32
NT = (((1,), (1,)), ((), ()))
VMEM_LIMIT = 63 << 20
CHUNK = 512
PIECES = 3
ROWS = 256
WINDOW = 256


def layer_norm(values, gain, shift):
    values = values.astype(F32)
    centred = values - jnp.mean(values, axis=-1, keepdims=True)
    var = jnp.mean(centred * centred, axis=-1, keepdims=True)
    return (centred * lax.rsqrt(var + LN_EPS) * gain + shift).astype(BF16)


def whole(shape):
    return pl.BlockSpec(shape, lambda i: (0,) * len(shape), pipeline_mode=pl.Buffered(1))


def layer_of(layer, shape):
    return pl.BlockSpec((None,) + shape, lambda i: (layer,) + (0,) * len(shape), pipeline_mode=pl.Buffered(1))


def project(normed_ref, w_ref, bias_row, out_ref, rows=512, cols=256):
    m, n_out = normed_ref.shape[0], w_ref.shape[0]

    def step(i, carry):
        at = pl.ds(pl.multiple_of(i * rows, rows), rows)
        normed = normed_ref[at, :]
        for c in range(0, n_out, cols):
            w = min(cols, n_out - c)
            y = lax.dot_general(normed, w_ref[c:c + w, :], NT, preferred_element_type=F32)
            out_ref[at, c:c + w] = (y + bias_row[:, c:c + w]).astype(BF16)
        return carry

    lax.fori_loop(0, m // rows, step, 0)


def qkv_kernel(x_ref, gain_ref, shift_ref, w_ref, bias_ref, out_ref, *, cols):
    normed = layer_norm(x_ref[...], gain_ref[0:1, :], shift_ref[0:1, :])
    n_out = w_ref.shape[0]
    for c in range(0, n_out, cols):
        w = min(cols, n_out - c)
        y = lax.dot_general(normed, w_ref[c:c + w, :], NT, preferred_element_type=F32)
        out_ref[:, c:c + w] = (y + bias_ref[0:1, c:c + w]).astype(BF16)
    out_ref[:, n_out:] = x_ref[...]


def qkv_call(x, start, m, gain, shift, w, bias, rows=512, cols=256):
    d = x.shape[1]
    n = w.shape[1]
    first = start // rows
    return pl.pallas_call(
        functools.partial(qkv_kernel, cols=cols),
        grid=(m // rows,),
        name="qkv",
        in_specs=[pl.BlockSpec((rows, d), lambda i: (first + i, 0)), whole(gain.shape), whole(shift.shape), layer_of(0, (n, d)), whole(bias.shape)],
        out_specs=pl.BlockSpec((rows, n + d), lambda i: (i, 0)),
        out_shape=jax.ShapeDtypeStruct((m, n + d), BF16),
        compiler_params=pltpu.CompilerParams(vmem_limit_bytes=VMEM_LIMIT),
        cost_estimate=pl.CostEstimate(flops=2 * m * d * n, bytes_accessed=2 * (2 * m * d + n * d + m * n), transcendentals=0),
    )(x, gain, shift, w, bias)


def attend(qkv_ref, out_ref, s_bufs, k_bufs, *, heads, head_dim, rows=512, unroll=2):
    seq = qkv_ref.shape[0]
    d = heads * head_dim
    blocks = seq // rows
    score_scale = (head_dim ** -0.5) * math.log2(math.e)

    def window(h):
        low = h * head_dim
        off = pl.multiple_of(jnp.minimum(low // 128, d // 128 - 2) * 128, 128)
        low = low - off
        lane = lax.broadcasted_iota(jnp.int32, (1, WINDOW), 1)
        return off, (lane >= low) & (lane < low + head_dim)

    def mask_keys(h, k_buf):
        off, mask = window(h)
        k = qkv_ref[:, pl.ds(pl.multiple_of(d + off, 128), WINDOW)]
        k_buf[...] = jnp.where(mask, k, jnp.zeros_like(k))

    def scores(h, j, s_buf, k_buf):
        off, _ = window(h)
        q = qkv_ref[j * rows:(j + 1) * rows, pl.ds(off, WINDOW)]
        s_buf[...] = lax.dot_general(q, k_buf[...], NT, preferred_element_type=F32)

    mask_keys(0, k_bufs[0])
    scores(0, 0, s_bufs[0], k_bufs[0])

    def some_heads(i, carry):
        t = 0
        for u in range(unroll):
            h = i * unroll + u
            off, mask = window(h)
            for j in range(blocks):
                if j + 1 < blocks:
                    scores(h, j + 1, s_bufs[(t + 1) % 2], k_bufs[u % 2])
                else:
                    after = jnp.minimum(h + 1, heads - 1)
                    mask_keys(after, k_bufs[(u + 1) % 2])
                    scores(after, 0, s_bufs[(t + 1) % 2], k_bufs[(u + 1) % 2])
                s = s_bufs[t % 2][...]
                peak = jnp.max(s, axis=-1, keepdims=True)
                p = jnp.exp2((s - peak) * score_scale)
                total = jnp.sum(p, axis=-1, keepdims=True)
                v = qkv_ref[:, pl.ds(pl.multiple_of(2 * d + off, 128), WINDOW)]
                o = jnp.dot(p.astype(BF16), v, preferred_element_type=F32)
                o = (o * (1.0 / total)).astype(BF16)
                place = (pl.ds(j * rows, rows), pl.ds(off, WINDOW))
                out_ref[place] = jnp.where(mask, o, out_ref[place])
                t += 1
        return carry

    lax.fori_loop(0, heads // unroll, some_heads, 0)


class Chunks:
    def __init__(self, hbm, vmem, sem, f):
        per = -(-f // (PIECES * CHUNK)) * CHUNK
        self.hbm, self.vmem, self.sem = hbm, vmem, sem
        self.bounds = [(p, min(per, f - p)) for p in range(0, f, per)]

    def copy(self, l, p):
        at = pl.ds(*self.bounds[p])
        return pltpu.make_async_copy(self.hbm.at[l, at, :], self.vmem.at[at, :], self.sem.at[p])

    def start(self, l):
        for p in range(len(self.bounds)):
            self.copy(l, p).start()

    def wait(self, l):
        for p in range(len(self.bounds)):
            self.copy(l, p).wait()


def mlp_block(l, at, h_ref, up, down, bu_ref, bd_ref, gain_ref, shift_ref, act_ref, streamed=False):
    row = pl.ds(l, 1)
    f = act_ref.shape[1]
    normed = layer_norm(h_ref[at, :], gain_ref[row, :], shift_ref[row, :])
    for p, (start, size) in enumerate(up.bounds):
        if streamed:
            up.copy(l, p).wait()
        for c in range(start, start + size, CHUNK):
            w = min(CHUNK, f - c)
            x = lax.dot_general(normed, up.vmem[c:c + w, :], NT, preferred_element_type=F32) + bu_ref[row, c:c + w]
            act_ref[:, c:c + w] = jax.nn.gelu(x, approximate=True).astype(BF16)
    y = h_ref[at, :].astype(F32) + bd_ref[row, :]
    if not streamed:
        return y + jnp.dot(act_ref[...], down.vmem[...], preferred_element_type=F32)
    for p, (start, size) in enumerate(down.bounds):
        down.copy(l, p).wait()
        y = y + jnp.dot(act_ref[:, start:start + size], down.vmem[start:start + size, :], preferred_element_type=F32)
    return y


def layers_kernel(*refs, projected, layers, heads, head_dim):
    (x_hbm, g1, s1, wi_hbm, bi, wo_hbm, bo, g2, s2, wu_hbm, bu, wd_hbm, bd, out_hbm,
     h, qkv, o, s_a, s_b, k_a, k_b, act, wi, wo, wu, wd, sem, up_sem, down_sem) = refs
    d = heads * head_dim
    f = wu.shape[0]
    up, down = Chunks(wu_hbm, wu, up_sem, f), Chunks(wd_hbm, wd, down_sem, f)
    wi_copy = lambda l: pltpu.make_async_copy(wi_hbm.at[l], wi, sem.at[0])
    wo_copy = lambda l: pltpu.make_async_copy(wo_hbm.at[l], wo, sem.at[1])
    if projected:
        h_copy = pltpu.make_async_copy(x_hbm.at[:, 3 * d:], h, sem.at[2])
        qkv_copy = pltpu.make_async_copy(x_hbm.at[:, :3 * d], qkv, sem.at[3])
        qkv_copy.start()
        h_copy.start()
        wo_copy(0).start()
        up.start(0)
        down.start(0)
        wi_copy(1).start()
        h_copy.wait()
        qkv_copy.wait()
    else:
        h_copy = pltpu.make_async_copy(x_hbm, h, sem.at[2])
        h_copy.start()
        wi_copy(0).start()
        wo_copy(0).start()
        up.start(0)
        down.start(0)
        h_copy.wait()
        o[...] = layer_norm(h[...], g1[0:1, :], s1[0:1, :])

    def layer(l, carry):
        def make_qkv():
            wi_copy(l).wait()
            project(o, wi, bi.at[pl.ds(l, 1), :], qkv)

            @pl.when(l + 1 < layers)
            def _():
                wi_copy(l + 1).start()

        if projected:
            pl.when(l > 0)(make_qkv)
        else:
            make_qkv()
        attend(qkv, o, (s_a, s_b), (k_a, k_b), heads=heads, head_dim=head_dim)
        wo_copy(l).wait()

        def out_proj(i, c):
            at = pl.ds(pl.multiple_of(i * 512, 512), 512)
            y = jnp.dot(o[at, :], wo[...], preferred_element_type=F32) + bo[pl.ds(l, 1), :]
            h[at, :] = (h[at, :].astype(F32) + y).astype(BF16)
            return c

        lax.fori_loop(0, h.shape[0] // 512, out_proj, 0)

        @pl.when(l + 1 < layers)
        def _():
            wo_copy(l + 1).start()

            def finish(at, y):
                y = y.astype(BF16)
                h[at, :] = y
                o[at, :] = layer_norm(y, g1[pl.ds(l + 1, 1), :], s1[pl.ds(l + 1, 1), :])

            up.wait(l)
            down.wait(l)

            def block(i, c):
                at = pl.ds(pl.multiple_of(i * ROWS, ROWS), ROWS)
                finish(at, mlp_block(l, at, h, up, down, bu, bd, g2, s2, act))
                return c

            lax.fori_loop(0, h.shape[0] // ROWS, block, 0)

            @pl.when(l + 2 < layers)
            def _():
                up.start(l + 1)
                down.start(l + 1)

        return carry

    lax.fori_loop(0, layers, layer, 0)
    out = pltpu.make_async_copy(h, out_hbm, sem.at[2])
    out.start()
    out.wait()


def layers_call(x, projected, params, heads, head_dim):
    g1, s1, wi, bi, wo, bo, g2, s2, wu, bu, wd, bd = params
    m = x.shape[0]
    layers, n, d = wi.shape
    f = wu.shape[1]
    any_spec = pl.BlockSpec(memory_space=pl.ANY)
    vmem = pl.BlockSpec(memory_space=pltpu.VMEM)
    flops = layers * m * (2 * d * (n + d) + 4 * m * d * 3) + (layers - 1) * m * 4 * d * f
    return pl.pallas_call(
        functools.partial(layers_kernel, projected=projected, layers=layers, heads=heads, head_dim=head_dim),
        name="layers",
        in_specs=[any_spec, vmem, vmem, any_spec, vmem, any_spec, vmem, vmem, vmem, any_spec, vmem, any_spec, vmem],
        out_specs=any_spec,
        out_shape=jax.ShapeDtypeStruct((m, d), BF16),
        scratch_shapes=[
            pltpu.VMEM((m, d), BF16), pltpu.VMEM((m, n), BF16), pltpu.VMEM((m, d), BF16),
            pltpu.VMEM((512, m), F32), pltpu.VMEM((512, m), F32), pltpu.VMEM((m, WINDOW), BF16), pltpu.VMEM((m, WINDOW), BF16),
            pltpu.VMEM((ROWS, f), BF16),
            pltpu.VMEM((n, d), BF16), pltpu.VMEM((d, d), BF16), pltpu.VMEM((f, d), BF16), pltpu.VMEM((f, d), BF16),
            pltpu.SemaphoreType.DMA((4,)), pltpu.SemaphoreType.DMA((PIECES,)), pltpu.SemaphoreType.DMA((PIECES,)),
        ],
        compiler_params=pltpu.CompilerParams(vmem_limit_bytes=VMEM_LIMIT),
        cost_estimate=pl.CostEstimate(flops=flops, bytes_accessed=2 * layers * d * (n + d + 2 * f), transcendentals=layers * heads * m * m),
    )(x, g1, s1, wi, bi, wo, bo, g2, s2, wu, bu, wd, bd)


def last_mlp_kernel(*refs, layer, start):
    m_hbm, g2, s2, wu_hbm, bu, wd_hbm, bd = refs[:7]
    out_hbm, h, out, act, wu, wd, h_sem, out_sem, up_sem, down_sem = refs[-10:]
    f = wu.shape[0]
    steps = h.shape[0] // ROWS
    up, down = Chunks(wu_hbm, wu, up_sem, f), Chunks(wd_hbm, wd, down_sem, f)
    first = pl.ds(0, ROWS)
    rest = pl.ds(ROWS, h.shape[0] - ROWS)
    copies = [pltpu.make_async_copy(m_hbm.at[at, :], h.at[at, :], h_sem.at[i]) for i, at in enumerate((first, rest))]
    copies[0].start()
    up.start(layer)
    copies[1].start()
    down.start(layer)

    def finish(i, streamed):
        at = pl.ds(pl.multiple_of(i * ROWS, ROWS), ROWS)
        y = mlp_block(layer, at, h, up, down, bu, bd, g2, s2, act, streamed)
        out[at, :] = y.astype(BF16)

    def write(i):
        at = pl.multiple_of(i * ROWS, ROWS)
        return pltpu.make_async_copy(out.at[pl.ds(at, ROWS), :], out_hbm.at[pl.ds(start + at, ROWS), :], out_sem.at[i])

    copies[0].wait()
    finish(0, True)
    write(0).start()
    copies[1].wait()

    def step(i, carry):
        finish(i, False)
        write(i).start()
        return carry

    lax.fori_loop(1, steps, step, 0)
    for i in range(steps):
        write(i).wait()


def last_mlp_call(layer, mid, params, total, start, into):
    g1, s1, wi, bi, wo, bo, g2, s2, wu, bu, wd, bd = params
    m, d = mid.shape
    f = wu.shape[1]
    any_spec = pl.BlockSpec(memory_space=pl.ANY)
    vmem = pl.BlockSpec(memory_space=pltpu.VMEM)
    args = [mid, g2, s2, wu, bu, wd, bd]
    specs = [any_spec, vmem, vmem, any_spec, vmem, any_spec, vmem]
    if into is not None:
        args.append(into)
        specs.append(any_spec)
    return pl.pallas_call(
        functools.partial(last_mlp_kernel, layer=layer, start=start),
        name="last_mlp",
        in_specs=specs,
        out_specs=any_spec,
        out_shape=jax.ShapeDtypeStruct((total, d), BF16),
        scratch_shapes=[
            pltpu.VMEM((m, d), BF16), pltpu.VMEM((m, d), BF16), pltpu.VMEM((ROWS, f), BF16), pltpu.VMEM((f, d), BF16), pltpu.VMEM((f, d), BF16),
            pltpu.SemaphoreType.DMA((2,)), pltpu.SemaphoreType.DMA((m // ROWS,)), pltpu.SemaphoreType.DMA((PIECES,)), pltpu.SemaphoreType.DMA((PIECES,)),
        ],
        input_output_aliases={7: 0} if into is not None else {},
        compiler_params=pltpu.CompilerParams(vmem_limit_bytes=VMEM_LIMIT),
        cost_estimate=pl.CostEstimate(flops=4 * m * d * f, bytes_accessed=4 * (m * d + f * d), transcendentals=m * f),
    )(*args)


def solution(mesh):
    token_spec = P('dp', 'sp', None)
    group = mesh.shape['sp']

    def device_step(image_tokens, ln1_gain, ln1_shift, w_qkv, b_qkv, w_out, b_out, ln2_gain, ln2_shift, w_up, b_up, w_down, b_down):
        images, tokens, d = image_tokens.shape
        layers, _, _, heads, head_dim = w_qkv.shape
        w_qkv_t = jnp.transpose(w_qkv, (0, 2, 3, 4, 1)).reshape(layers, 3 * d, d)
        params = (ln1_gain, ln1_shift, w_qkv_t, b_qkv.reshape(layers, 3 * d), w_out.reshape(layers, d, d), b_out,
                  ln2_gain, ln2_shift, jnp.transpose(w_up, (0, 2, 1)), b_up, w_down, b_down)
        rounds = images // group
        part = group * tokens

        def exchange(rows):
            blocks = rows.reshape(group, tokens, rows.shape[-1])
            return lax.all_to_all(blocks, 'sp', 0, 0, tiled=True).reshape(part, rows.shape[-1])

        own = image_tokens.reshape(rounds * part, d)
        moved = [exchange(own[:part])]
        for r in range(1, rounds):
            moved.append(exchange(qkv_call(own, r * part, part, ln1_gain, ln1_shift, w_qkv_t, params[3])))
        mids = [exchange(layers_call(moved[r], r > 0, params, heads, head_dim)) for r in range(rounds)]
        out = None
        for r in range(rounds):
            out = last_mlp_call(layers - 1, mids[r], params, rounds * part, r * part, out)
        return out.reshape(images, tokens, d)

    return jax.shard_map(device_step, mesh=mesh, in_specs=(token_spec,) + (P(),) * 12, out_specs=token_spec, check_vma=False)
```

time: 407 us -> 343 us (0.84)
  Pallas kernels: 352 us -> 299 us
  local copies, waits for them, and re-layouts: 10 us -> 3.99 us
  starting transfers between devices: 27.2 us -> 22 us
    pallas_call x16 -> x5, Pallas kernels: 352 us -> 299 us  [the longest x2 217 us: layers_call(): pl.pallas_call(functools.partial(layers_kernel, projected=projected, laye...]
    all_to_all x5 -> x4, starting transfers between devices: 27.2 us -> 22 us  [exchange(): lax.all_to_all(blocks, 'sp', 0, 0, tiled=True).reshape(part, rows.shape[-1])]
    unnamed x8 -> x2, local copies, waits for them, and re-layouts: 4.23 us -> 0.01 us
    all_to_all x5 -> x4, waiting for transfers between devices: 11.8 us -> 11.6 us  [exchange(): lax.all_to_all(blocks, 'sp', 0, 0, tiled=True).reshape(part, rows.shape[-1])]
  transfers between devices with their start and end apart: 5 -> 4, of which waited for: 1 -> 1; matrix products, arithmetic and copies ran while one was open for 0% -> 0% of each run, Pallas kernels for 79% -> 79%
where the time goes in v2:
time: 343 us; the launch traced here: 337 us
  Pallas kernels  299 us (87%)
  starting transfers between devices  22 us (6%)
  waiting for transfers between devices  11.6 us (3%)
  local copies, waits for them, and re-layouts  3.99 us (1%)
    pallas_call x2, Pallas kernels, layers_call(): pl.pallas_call(functools.partial(layers_kernel, projected=projected, laye...  217 us
    pallas_call x2, Pallas kernels, last_mlp_call(): pl.pallas_call(functools.partial(last_mlp_kernel, layer=layer, start=star...  65.4 us
    all_to_all x4, starting transfers between devices, exchange(): lax.all_to_all(blocks, 'sp', 0, 0, tiled=True).reshape(part, rows.shape[-1])  22 us
    pallas_call x1, Pallas kernels, qkv_call(): pl.pallas_call(functools.partial(qkv_kernel, cols=cols), grid=(m // rows,...  16.7 us
    all_to_all x4, waiting for transfers between devices, exchange(): lax.all_to_all(blocks, 'sp', 0, 0, tiled=True).reshape(part, rows.shape[-1])  11.6 us
  transfers between devices with their start and end apart: 4, of which 1 were waited for; matrix products, arithmetic and copies ran while one was open for 0% of the time, Pallas kernels for 79%

profile of v2, /device:TPU:81, one launch (start us, length us, event | category | flops | bytes accessed | tf_op | source)
XLA Modules:
  0.0 337.2 jit_solution(16183242917377616857)
XLA Ops:
  0.0 0.0 copy-start
  0.0 3.3 slice.4
  3.3 6.3 %all-to-all-start.2 = ((bf16[8,128,1152]{2,1,0:T(8,128)(2,1)}), bf16[8,128,1152]{2,1,0:T(8,128)(2,1)}, u32[]{:S(2)}, u32[]{:S(2)}) async-start(bf16[8,128,1152]{2,1,0:T(8,128)(2,1)} %slice.4), calls=%async_computation.2 | async-start | bytes 4718592 | tf_op jit(solution)/shard_map/all_to_all | solution.py:361
  9.6 0.0 copy-done
  9.6 0.7 reshape.41.bias_ref.refs_4_
  10.3 16.7 %qkv.1 = bf16[1024,4608]{1,0:T(8,128)(2,1)} custom-call(bf16[2048,1152]{1,0:T(8,128)(2,1)} %bitcast.19, f32[2,1152]{1,0:T(2,128)} %refs_1_.5, f32[2,1152]{1,0:T(2,128)} %refs_2_.5, bf16[2,3456,1152]{2,1,0:T(8,128)(2,1)} %bitcast.24, f32[2,3456]{1,0:T(2,128)} %reshape.41.bias_ref.refs_4_), custom_call_target="tpu_custom_call" | custom-call | flops 8153726976 | bytes 19759104 | tf_op jit(solution)/shard_map/qkv/pallas_call | solution.py:66
  27.0 11.6 %all-to-all-done.2 = bf16[8,128,1152]{2,1,0:T(8,128)(2,1)} async-done(((bf16[8,128,1152]{2,1,0:T(8,128)(2,1)}), bf16[8,128,1152]{2,1,0:T(8,128)(2,1)}, u32[]{:S(2)}, u32[]{:S(2)}) %all-to-all-start.2) | async-done | bytes 2359328 | tf_op jit(solution)/shard_map/all_to_all | solution.py:361
  38.6 6.0 %all-to-all-start = ((bf16[8,128,4608]{2,1,0:T(8,128)(2,1)}), bf16[8,128,4608]{2,1,0:T(8,128)(2,1)}, u32[]{:S(2)}, u32[]{:S(2)}) async-start(bf16[8,128,4608]{2,1,0:T(8,128)(2,1)} %bitcast.16), calls=%async_computation | async-start | bytes 18874368 | tf_op jit(solution)/shard_map/all_to_all | solution.py:361
  44.6 114.3 %layers.3 = bf16[1024,1152]{1,0:T(8,128)(2,1)} custom-call(bf16[1024,1152]{1,0:T(8,128)(2,1)} %bitcast.9.refs_0_, f32[2,1152]{1,0:T(2,128)} %refs_1_.5, f32[2,1152]{1,0:T(2,128)} %refs_2_.5, bf16[2,3456,1152]{2,1,0:T(8,128)(2,1)} %bitcast.25, f32[2,3456]{1,0:T(2,128)} %reshape.41.bias_ref.refs_4_, bf16[2,1152,1152]{2,1,0:T(8,128)(2,1)} %bitcast.27, ...), custom_call_target="tpu_custom_call" | custom-call | flops 71043121152 | bytes 60899328 | tf_op jit(solution)/shard_map/layers/pallas_call | solution.py:263
  158.9 0.0 all-to-all-done
  158.9 4.9 %all-to-all-start.3 = ((bf16[8,128,1152]{2,1,0:T(8,128)(2,1)}), bf16[8,128,1152]{2,1,0:T(8,128)(2,1)}, u32[]{:S(2)}, u32[]{:S(2)}) async-start(bf16[8,128,1152]{2,1,0:T(8,128)(2,1)} %bitcast.17), calls=%async_computation.3 | async-start | bytes 4718592 | tf_op jit(solution)/shard_map/all_to_all | solution.py:361
  163.8 102.9 %layers.2 = bf16[1024,1152]{1,0:T(8,128)(2,1)} custom-call(bf16[1024,4608]{1,0:T(8,128)(2,1)} %bitcast.4.refs_0_, f32[2,1152]{1,0:T(2,128)} %refs_1_.5, f32[2,1152]{1,0:T(2,128)} %refs_2_.5, bf16[2,3456,1152]{2,1,0:T(8,128)(2,1)} %bitcast.26, f32[2,3456]{1,0:T(2,128)} %reshape.41.bias_ref.refs_4_, bf16[2,1152,1152]{2,1,0:T(8,128)(2,1)} %bitcast.28, ...), custom_call_target="tpu_custom_call" | custom-call | flops 71043121152 | bytes 60899328 | tf_op jit(solution)/shard_map/layers/pallas_call | solution.py:263
  266.7 0.0 all-to-all-done.3
  266.7 4.8 %all-to-all-start.1 = ((bf16[8,128,1152]{2,1,0:T(8,128)(2,1)}), bf16[8,128,1152]{2,1,0:T(8,128)(2,1)}, u32[]{:S(2)}, u32[]{:S(2)}) async-start(bf16[8,128,1152]{2,1,0:T(8,128)(2,1)} %bitcast.18), calls=%async_computation.1 | async-start | bytes 4718592 | tf_op jit(solution)/shard_map/all_to_all | solution.py:361
  271.6 32.7 %last_mlp.2.refs_7_ = bf16[2048,1152]{1,0:T(8,128)(2,1)} custom-call(bf16[1024,1152]{1,0:T(8,128)(2,1)} %bitcast.12.refs_0_, f32[2,1152]{1,0:T(2,128)} %refs_1_.7, f32[2,1152]{1,0:T(2,128)} %refs_2_.7, bf16[2,4304,1152]{2,1,0:T(8,128)(2,1)} %bitcast.22, f32[2,4304]{1,0:T(2,128)} %refs_4_.3, bf16[2,4304,1152]{2,1,0:T(8,128)(2,1)} %refs_5_.3, f32[2,1152]{1,0:T(2,128)} %refs_6_.7), custom_call_target="tpu_custom_call" | custom-call | flops 20308819968 | bytes 24551424 | tf_op jit(solution)/shard_map/last_mlp/pallas_call | solution.py:330
  304.3 0.0 all-to-all-done.1
  304.3 32.7 %last_mlp.3 = bf16[2048,1152]{1,0:T(8,128)(2,1)} custom-call(bf16[1024,1152]{1,0:T(8,128)(2,1)} %bitcast.8.refs_0_, f32[2,1152]{1,0:T(2,128)} %refs_1_.7, f32[2,1152]{1,0:T(2,128)} %refs_2_.7, bf16[2,4304,1152]{2,1,0:T(8,128)(2,1)} %bitcast.23, f32[2,4304]{1,0:T(2,128)} %refs_4_.3, bf16[2,4304,1152]{2,1,0:T(8,128)(2,1)} %refs_5_.3, ...), custom_call_target="tpu_custom_call", output_to_operand_aliasing={{}: (7, {})} | custom-call | flops 20308819968 | bytes 24551424 | tf_op jit(solution)/shard_map/last_mlp/pallas_call | solution.py:330
Async XLA Ops:
  0.0 9.6 %copy-start = (f32[2,3,16,72]{3,2,1,0:T(8,128)S(1)}, f32[2,3,16,72]{3,2,1,0:T(8,128)}, u32[]{:S(2)}) copy-start(f32[2,3,16,72]{3,2,1,0:T(8,128)} %param.17) | copy-start | bytes 82948
  3.3 35.3 %all-to-all-start.2 = ((bf16[8,128,1152]{2,1,0:T(8,128)(2,1)}), bf16[8,128,1152]{2,1,0:T(8,128)(2,1)}, u32[]{:S(2)}, u32[]{:S(2)}) async-start(bf16[8,128,1152]{2,1,0:T(8,128)(2,1)} %slice.4), calls=%async_computation.2 | async-start | bytes 4718592 | tf_op jit(solution)/shard_map/all_to_all | solution.py:361
  38.6 120.4 %all-to-all-start = ((bf16[8,128,4608]{2,1,0:T(8,128)(2,1)}), bf16[8,128,4608]{2,1,0:T(8,128)(2,1)}, u32[]{:S(2)}, u32[]{:S(2)}) async-start(bf16[8,128,4608]{2,1,0:T(8,128)(2,1)} %bitcast.16), calls=%async_computation | async-start | bytes 18874368 | tf_op jit(solution)/shard_map/all_to_all | solution.py:361
  158.9 107.8 %all-to-all-start.3 = ((bf16[8,128,1152]{2,1,0:T(8,128)(2,1)}), bf16[8,128,1152]{2,1,0:T(8,128)(2,1)}, u32[]{:S(2)}, u32[]{:S(2)}) async-start(bf16[8,128,1152]{2,1,0:T(8,128)(2,1)} %bitcast.17), calls=%async_computation.3 | async-start | bytes 4718592 | tf_op jit(solution)/shard_map/all_to_all | solution.py:361
  266.7 37.6 %all-to-all-start.1 = ((bf16[8,128,1152]{2,1,0:T(8,128)(2,1)}), bf16[8,128,1152]{2,1,0:T(8,128)(2,1)}, u32[]{:S(2)}, u32[]{:S(2)}) async-start(bf16[8,128,1152]{2,1,0:T(8,128)(2,1)} %bitcast.18), calls=%async_computation.1 | async-start | bytes 4718592 | tf_op jit(solution)/shard_map/all_to_all | solution.py:361

commit v3 on v2

--- a/solution.py
+++ b/solution.py
@@ -16,6 +16,7 @@
 CHUNK = 512
 PIECES = 3
 ROWS = 256
+AHEAD = 2
 WINDOW = 256
 
 
@@ -151,9 +152,18 @@
     row = pl.ds(l, 1)
     f = act_ref.shape[1]
     normed = layer_norm(h_ref[at, :], gain_ref[row, :], shift_ref[row, :])
+    pieces = [(w, p) for w in (up, down) for p in range(len(w.bounds))]
+
+    def arrive(k):
+        w, p = pieces[k]
+        w.copy(l, p).wait()
+        if k + AHEAD < len(pieces):
+            w, p = pieces[k + AHEAD]
+            w.copy(l, p).start()
+
     for p, (start, size) in enumerate(up.bounds):
         if streamed:
-            up.copy(l, p).wait()
+            arrive(p)
         for c in range(start, start + size, CHUNK):
             w = min(CHUNK, f - c)
             x = lax.dot_general(normed, up.vmem[c:c + w, :], NT, preferred_element_type=F32) + bu_ref[row, c:c + w]
@@ -162,7 +172,7 @@
     if not streamed:
         return y + jnp.dot(act_ref[...], down.vmem[...], preferred_element_type=F32)
     for p, (start, size) in enumerate(down.bounds):
-        down.copy(l, p).wait()
+        arrive(len(up.bounds) + p)
         y = y + jnp.dot(act_ref[:, start:start + size], down.vmem[start:start + size, :], preferred_element_type=F32)
     return y
 
@@ -179,26 +189,30 @@
         h_copy = pltpu.make_async_copy(x_hbm.at[:, 3 * d:], h, sem.at[2])
         qkv_copy = pltpu.make_async_copy(x_hbm.at[:, :3 * d], qkv, sem.at[3])
         qkv_copy.start()
+        qkv_copy.wait()
         h_copy.start()
         wo_copy(0).start()
         up.start(0)
         down.start(0)
         wi_copy(1).start()
-        h_copy.wait()
-        qkv_copy.wait()
     else:
         h_copy = pltpu.make_async_copy(x_hbm, h, sem.at[2])
         h_copy.start()
         wi_copy(0).start()
-        wo_copy(0).start()
-        up.start(0)
-        down.start(0)
         h_copy.wait()
         o[...] = layer_norm(h[...], g1[0:1, :], s1[0:1, :])
 
     def layer(l, carry):
         def make_qkv():
             wi_copy(l).wait()
+            if not projected:
+
+                @pl.when(l == 0)
+                def _():
+                    wo_copy(0).start()
+                    up.start(0)
+                    down.start(0)
+
             project(o, wi, bi.at[pl.ds(l, 1), :], qkv)
 
             @pl.when(l + 1 < layers)
@@ -209,8 +223,10 @@
             pl.when(l > 0)(make_qkv)
         else:
             make_qkv()
-        attend(qkv, o, (s_a, s_b), (k_a, k_b), heads=heads, head_dim=head_dim)
+        attend(qkv, o, (s_a, s_b), (k_a, k_b), heads=heads, head_dim=head_dim, unroll=4 if projected else 2)
         wo_copy(l).wait()
+        if projected:
+            pl.when(l == 0)(h_copy.wait)
 
         def out_proj(i, c):
             at = pl.ds(pl.multiple_of(i * 512, 512), 512)
@@ -288,9 +304,8 @@
     rest = pl.ds(ROWS, h.shape[0] - ROWS)
     copies = [pltpu.make_async_copy(m_hbm.at[at, :], h.at[at, :], h_sem.at[i]) for i, at in enumerate((first, rest))]
     copies[0].start()
-    up.start(layer)
-    copies[1].start()
-    down.start(layer)
+    for p in range(AHEAD):
+        up.copy(layer, p).start()
 
     def finish(i, streamed):
         at = pl.ds(pl.multiple_of(i * ROWS, ROWS), ROWS)
@@ -302,6 +317,7 @@
         return pltpu.make_async_copy(out.at[pl.ds(at, ROWS), :], out_hbm.at[pl.ds(start + at, ROWS), :], out_sem.at[i])
 
     copies[0].wait()
+    copies[1].start()
     finish(0, True)
     write(0).start()
     copies[1].wait()

time: 343 us -> 337 us (0.983)
  Pallas kernels: 299 us -> 293 us
    pallas_call x2, Pallas kernels: 217 us -> 213 us  [layers_call(): pl.pallas_call(functools.partial(layers_kernel, projected=projected, laye...]
where the time goes in v3:
time: 337 us; the launch traced here: 331 us
  Pallas kernels  293 us (87%)
  starting transfers between devices  22 us (7%)
  waiting for transfers between devices  11.6 us (3%)
  local copies, waits for them, and re-layouts  3.99 us (1%)
    pallas_call x2, Pallas kernels, layers_call(): pl.pallas_call(functools.partial(layers_kernel, projected=projected, laye...  213 us
    pallas_call x2, Pallas kernels, last_mlp_call(): pl.pallas_call(functools.partial(last_mlp_kernel, layer=layer, start=star...  63.4 us
    all_to_all x4, starting transfers between devices, exchange(): lax.all_to_all(blocks, 'sp', 0, 0, tiled=True).reshape(part, rows.shape[-1])  22 us
    pallas_call x1, Pallas kernels, qkv_call(): pl.pallas_call(functools.partial(qkv_kernel, cols=cols), grid=(m // rows,...  16.7 us
    all_to_all x4, waiting for transfers between devices, exchange(): lax.all_to_all(blocks, 'sp', 0, 0, tiled=True).reshape(part, rows.shape[-1])  11.6 us
  transfers between devices with their start and end apart: 4, of which 1 were waited for; matrix products, arithmetic and copies ran while one was open for 0% of the time, Pallas kernels for 79%

profile of v3, /device:TPU:81, one launch (start us, length us, event | category | flops | bytes accessed | tf_op | source)
XLA Modules:
  0.0 330.6 jit_solution(7311525723577352649)
XLA Ops:
  0.0 0.0 copy-start
  0.0 3.3 slice.4
  3.3 6.3 %all-to-all-start.2 = ((bf16[8,128,1152]{2,1,0:T(8,128)(2,1)}), bf16[8,128,1152]{2,1,0:T(8,128)(2,1)}, u32[]{:S(2)}, u32[]{:S(2)}) async-start(bf16[8,128,1152]{2,1,0:T(8,128)(2,1)} %slice.4), calls=%async_computation.2 | async-start | bytes 4718592 | tf_op jit(solution)/shard_map/all_to_all | solution.py:377
  9.6 0.0 copy-done
  9.6 0.7 reshape.41.bias_ref.refs_4_
  10.3 16.7 %qkv.1 = bf16[1024,4608]{1,0:T(8,128)(2,1)} custom-call(bf16[2048,1152]{1,0:T(8,128)(2,1)} %bitcast.19, f32[2,1152]{1,0:T(2,128)} %refs_1_.5, f32[2,1152]{1,0:T(2,128)} %refs_2_.5, bf16[2,3456,1152]{2,1,0:T(8,128)(2,1)} %bitcast.24, f32[2,3456]{1,0:T(2,128)} %reshape.41.bias_ref.refs_4_), custom_call_target="tpu_custom_call" | custom-call | flops 8153726976 | bytes 19759104 | tf_op jit(solution)/shard_map/qkv/pallas_call | solution.py:67
  27.0 11.6 %all-to-all-done.2 = bf16[8,128,1152]{2,1,0:T(8,128)(2,1)} async-done(((bf16[8,128,1152]{2,1,0:T(8,128)(2,1)}), bf16[8,128,1152]{2,1,0:T(8,128)(2,1)}, u32[]{:S(2)}, u32[]{:S(2)}) %all-to-all-start.2) | async-done | bytes 2359328 | tf_op jit(solution)/shard_map/all_to_all | solution.py:377
  38.6 6.0 %all-to-all-start = ((bf16[8,128,4608]{2,1,0:T(8,128)(2,1)}), bf16[8,128,4608]{2,1,0:T(8,128)(2,1)}, u32[]{:S(2)}, u32[]{:S(2)}) async-start(bf16[8,128,4608]{2,1,0:T(8,128)(2,1)} %bitcast.16), calls=%async_computation | async-start | bytes 18874368 | tf_op jit(solution)/shard_map/all_to_all | solution.py:377
  44.6 112.3 %layers.3 = bf16[1024,1152]{1,0:T(8,128)(2,1)} custom-call(bf16[1024,1152]{1,0:T(8,128)(2,1)} %bitcast.9.refs_0_, f32[2,1152]{1,0:T(2,128)} %refs_1_.5, f32[2,1152]{1,0:T(2,128)} %refs_2_.5, bf16[2,3456,1152]{2,1,0:T(8,128)(2,1)} %bitcast.25, f32[2,3456]{1,0:T(2,128)} %reshape.41.bias_ref.refs_4_, bf16[2,1152,1152]{2,1,0:T(8,128)(2,1)} %bitcast.27, ...), custom_call_target="tpu_custom_call" | custom-call | flops 71043121152 | bytes 60899328 | tf_op jit(solution)/shard_map/layers/pallas_call | solution.py:279
  156.9 0.0 all-to-all-done
  156.9 4.9 %all-to-all-start.3 = ((bf16[8,128,1152]{2,1,0:T(8,128)(2,1)}), bf16[8,128,1152]{2,1,0:T(8,128)(2,1)}, u32[]{:S(2)}, u32[]{:S(2)}) async-start(bf16[8,128,1152]{2,1,0:T(8,128)(2,1)} %bitcast.17), calls=%async_computation.3 | async-start | bytes 4718592 | tf_op jit(solution)/shard_map/all_to_all | solution.py:377
  161.8 100.3 %layers.2 = bf16[1024,1152]{1,0:T(8,128)(2,1)} custom-call(bf16[1024,4608]{1,0:T(8,128)(2,1)} %bitcast.4.refs_0_, f32[2,1152]{1,0:T(2,128)} %refs_1_.5, f32[2,1152]{1,0:T(2,128)} %refs_2_.5, bf16[2,3456,1152]{2,1,0:T(8,128)(2,1)} %bitcast.26, f32[2,3456]{1,0:T(2,128)} %reshape.41.bias_ref.refs_4_, bf16[2,1152,1152]{2,1,0:T(8,128)(2,1)} %bitcast.28, ...), custom_call_target="tpu_custom_call" | custom-call | flops 71043121152 | bytes 60899328 | tf_op jit(solution)/shard_map/layers/pallas_call | solution.py:279
  262.1 0.0 all-to-all-done.3
  262.1 4.8 %all-to-all-start.1 = ((bf16[8,128,1152]{2,1,0:T(8,128)(2,1)}), bf16[8,128,1152]{2,1,0:T(8,128)(2,1)}, u32[]{:S(2)}, u32[]{:S(2)}) async-start(bf16[8,128,1152]{2,1,0:T(8,128)(2,1)} %bitcast.18), calls=%async_computation.1 | async-start | bytes 4718592 | tf_op jit(solution)/shard_map/all_to_all | solution.py:377
  267.0 31.7 %last_mlp.2.refs_7_ = bf16[2048,1152]{1,0:T(8,128)(2,1)} custom-call(bf16[1024,1152]{1,0:T(8,128)(2,1)} %bitcast.12.refs_0_, f32[2,1152]{1,0:T(2,128)} %refs_1_.7, f32[2,1152]{1,0:T(2,128)} %refs_2_.7, bf16[2,4304,1152]{2,1,0:T(8,128)(2,1)} %bitcast.22, f32[2,4304]{1,0:T(2,128)} %refs_4_.3, bf16[2,4304,1152]{2,1,0:T(8,128)(2,1)} %refs_5_.3, f32[2,1152]{1,0:T(2,128)} %refs_6_.7), custom_call_target="tpu_custom_call" | custom-call | flops 20308819968 | bytes 24551424 | tf_op jit(solution)/shard_map/last_mlp/pallas_call | solution.py:346
  298.7 0.0 all-to-all-done.1
  298.7 31.7 %last_mlp.3 = bf16[2048,1152]{1,0:T(8,128)(2,1)} custom-call(bf16[1024,1152]{1,0:T(8,128)(2,1)} %bitcast.8.refs_0_, f32[2,1152]{1,0:T(2,128)} %refs_1_.7, f32[2,1152]{1,0:T(2,128)} %refs_2_.7, bf16[2,4304,1152]{2,1,0:T(8,128)(2,1)} %bitcast.23, f32[2,4304]{1,0:T(2,128)} %refs_4_.3, bf16[2,4304,1152]{2,1,0:T(8,128)(2,1)} %refs_5_.3, ...), custom_call_target="tpu_custom_call", output_to_operand_aliasing={{}: (7, {})} | custom-call | flops 20308819968 | bytes 24551424 | tf_op jit(solution)/shard_map/last_mlp/pallas_call | solution.py:346
Async XLA Ops:
  0.0 9.6 %copy-start = (f32[2,3,16,72]{3,2,1,0:T(8,128)S(1)}, f32[2,3,16,72]{3,2,1,0:T(8,128)}, u32[]{:S(2)}) copy-start(f32[2,3,16,72]{3,2,1,0:T(8,128)} %param.17) | copy-start | bytes 82948
  3.3 35.3 %all-to-all-start.2 = ((bf16[8,128,1152]{2,1,0:T(8,128)(2,1)}), bf16[8,128,1152]{2,1,0:T(8,128)(2,1)}, u32[]{:S(2)}, u32[]{:S(2)}) async-start(bf16[8,128,1152]{2,1,0:T(8,128)(2,1)} %slice.4), calls=%async_computation.2 | async-start | bytes 4718592 | tf_op jit(solution)/shard_map/all_to_all | solution.py:377
  38.6 118.3 %all-to-all-start = ((bf16[8,128,4608]{2,1,0:T(8,128)(2,1)}), bf16[8,128,4608]{2,1,0:T(8,128)(2,1)}, u32[]{:S(2)}, u32[]{:S(2)}) async-start(bf16[8,128,4608]{2,1,0:T(8,128)(2,1)} %bitcast.16), calls=%async_computation | async-start | bytes 18874368 | tf_op jit(solution)/shard_map/all_to_all | solution.py:377
  156.9 105.2 %all-to-all-start.3 = ((bf16[8,128,1152]{2,1,0:T(8,128)(2,1)}), bf16[8,128,1152]{2,1,0:T(8,128)(2,1)}, u32[]{:S(2)}, u32[]{:S(2)}) async-start(bf16[8,128,1152]{2,1,0:T(8,128)(2,1)} %bitcast.17), calls=%async_computation.3 | async-start | bytes 4718592 | tf_op jit(solution)/shard_map/all_to_all | solution.py:377
  262.1 36.5 %all-to-all-start.1 = ((bf16[8,128,1152]{2,1,0:T(8,128)(2,1)}), bf16[8,128,1152]{2,1,0:T(8,128)(2,1)}, u32[]{:S(2)}, u32[]{:S(2)}) async-start(bf16[8,128,1152]{2,1,0:T(8,128)(2,1)} %bitcast.18), calls=%async_computation.1 | async-start | bytes 4718592 | tf_op jit(solution)/shard_map/all_to_all | solution.py:377
